TPU v7x, 32 devices: a whole 2x2x4 slice. The times are simulated.
32 devices in a mesh: rows: 8 (over z, x), grp: 4 (over y, core).
Axes of the slice: x: 2, y: 2, z: 4, core: 2. Of those that a mesh axis runs over, the one named last changes fastest.
Arguments:
- user_features: bfloat16 [4, 2048, 256], P('grp', 'rows'), may hold values from -72 to 72
- w_first: bfloat16 [256, 256], replicated, may hold values from -0.375 to 0.375
- w_second: bfloat16 [256, 256], replicated, may hold values from -0.375 to 0.375
- item_embed: bfloat16 [4, 2048, 256], P('grp', 'rows'), may hold values from -27 to 27
- example_weight: float32 [4, 2048], P('grp', 'rows'), may hold values from 0.02 to 0.2
- positive: int32 [4, 2048], P('grp', 'rows'), may hold values from 0 to 2047
- item_owner: int32 [4, 2048, 1], P('grp', 'rows'), may hold values from 0 to 7; in each aligned block of 256 rows (0 to 255, 256 to 511, ..., all dimensions but the last counted through in order) at most 128 rows name the same one
- item_row: int32 [4, 2048], P('grp', 'rows'), may hold values from 0 to 4095
Outputs:
- grad_first: float32 [256, 256], replicated
- grad_second: float32 [256, 256], replicated
- grad_table: float32 [32768, 256], P('rows', 'grp')
Inputs may be any that keep to these rules, and one draw needn't show every extreme that they name: `item_owner`: within the rows of one device (aligned blocks of 256 pairs of a group) no owner is named by more than 128 pairs, a bound that some block reaches.
All inputs are finite; a program needn't handle non-finite values.
Results may differ from a plain program's by a relative error of at most 0.0023.
The roundings to bfloat16 on the way count: a program that leaves them out, or rounds other values in their place, can miss the bound.
Values may be sent and summed in bfloat16 or wider, within the bound.
A program may use at most 128 MiB of HBM per device.

v0:
```python
import jax
import jax.numpy as jnp
from jax import lax
from jax.sharding import PartitionSpec as P

ITEMS_DEV = 4096


def contract_first(left, right):
    return lax.dot_general(
        left, right, (((0,), (0,)), ((), ())), preferred_element_type=jnp.float32
    )


def contract_last(left, right):
    return lax.dot_general(
        left, right, (((1,), (1,)), ((), ())), preferred_element_type=jnp.float32
    )


def body(
    user_features, w_first, w_second, item_embed, example_weight, positive, item_owner, item_row
):
    features = user_features[0]
    own_items = item_embed[0]
    weights = example_weight[0]
    targets = positive[0]
    owners = item_owner[0, :, 0]
    item_rows = item_row[0]
    my_users = features.shape[0]
    feature_width = own_items.shape[1]
    peers = lax.axis_size("rows")
    my_index = lax.axis_index("rows")
    pre_act = jnp.dot(features, w_first, preferred_element_type=jnp.float32)
    hidden = jax.nn.silu(pre_act).astype(jnp.bfloat16)
    user_vecs = jnp.dot(hidden, w_second, preferred_element_type=jnp.float32).astype(jnp.bfloat16)
    gathered = lax.all_gather(own_items, "rows", axis=0, tiled=True)
    group_users = gathered.shape[0]
    scores = contract_last(user_vecs, gathered)
    row_max = jnp.max(scores, axis=1, keepdims=True)
    log_total = row_max + jnp.log(jnp.sum(jnp.exp(scores - row_max), axis=1, keepdims=True))
    columns = lax.broadcasted_iota(jnp.int32, (1, group_users), 1)
    chosen = (columns == targets[:, None]).astype(jnp.float32)
    dscore = (weights[:, None] * (jnp.exp(scores - log_total) - chosen)).astype(jnp.bfloat16)
    grad_user = jnp.dot(dscore, gathered, preferred_element_type=jnp.float32).astype(jnp.bfloat16)
    everyone = lax.all_gather(user_vecs, "rows", axis=0, tiled=True)
    target_all, total_all, weight_all = (
        lax.all_gather(targets.astype(jnp.float32), "rows", axis=0, tiled=True),
        lax.all_gather(log_total[:, 0], "rows", axis=0, tiled=True),
        lax.all_gather(weights, "rows", axis=0, tiled=True),
    )
    back_scores = contract_last(everyone, own_items)
    own_columns = my_index * my_users + lax.broadcasted_iota(jnp.int32, (1, my_users), 1)
    hits = (own_columns == target_all.astype(jnp.int32)[:, None]).astype(jnp.float32)
    back_dscore = (weight_all[:, None] * (jnp.exp(back_scores - total_all[:, None]) - hits)).astype(
        jnp.bfloat16
    )
    grad_item = contract_first(back_dscore, everyone)
    d_second = contract_first(hidden, grad_user)
    back_grad = contract_last(grad_user, w_second)
    sigmoid_pre = jax.nn.sigmoid(pre_act)
    grad_pre = (back_grad * sigmoid_pre * (1.0 + pre_act * (1.0 - sigmoid_pre))).astype(
        jnp.bfloat16
    )
    d_first = contract_first(features, grad_pre)
    grad_first, grad_second = lax.psum((d_first, d_second), ("rows", "grp"))
    capacity = max(2, 4 * my_users // peers)
    member = (owners[:, None] == lax.broadcasted_iota(jnp.int32, (1, peers), 1)).astype(jnp.int32)
    before = jnp.cumsum(member, axis=0) - member
    slot_rank = jnp.sum(before * member, axis=1)
    slots = owners * capacity + slot_rank
    send_grad = jnp.zeros((peers * capacity, feature_width), jnp.float32).at[slots].set(grad_item)
    send_grad = send_grad.reshape(peers, capacity, feature_width)
    send_rows = (
        jnp.full((peers * capacity,), -1.0, jnp.float32)
        .at[slots]
        .set(item_rows.astype(jnp.float32))
    )
    got_grad, got_rows = (
        lax.all_to_all(send_grad, "rows", split_axis=0, concat_axis=0, tiled=True),
        lax.all_to_all(
            send_rows.reshape(peers, capacity), "rows", split_axis=0, concat_axis=0, tiled=True
        ),
    )
    table_rows = got_rows.reshape(-1).astype(jnp.int32)
    table_rows = jnp.where(table_rows >= 0, table_rows, ITEMS_DEV)
    dense_grad = (
        jnp.zeros((ITEMS_DEV, feature_width), jnp.float32)
        .at[table_rows]
        .add(got_grad.reshape(-1, feature_width), mode="drop")
    )
    grad_table = lax.psum_scatter(dense_grad, "grp", scatter_dimension=1, tiled=True)
    return (grad_first, grad_second, grad_table)


def solution(mesh):
    placed = (
        P("grp", "rows", None),
        P(),
        P(),
        P("grp", "rows", None),
        P("grp", "rows"),
        P("grp", "rows"),
        P("grp", "rows", None),
        P("grp", "rows"),
    )
    return jax.shard_map(
        body, mesh=mesh, in_specs=placed, out_specs=(P(), P(), P("rows", "grp")), check_vma=False
    )
```

profile of v0, /device:TPU:0, one launch (start us, length us, event | category | flops | bytes accessed | tf_op | source)
XLA Modules:
  0.0 301.3 jit_solution(13880731240005856503)
XLA Ops:
  7.2 0.0 copy-start
  7.2 0.0 copy-start.3
  7.2 0.0 copy-start.5
  7.2 0.0 copy-start.4
  7.2 0.0 all-gather.9.cloned.1.call-start
  7.3 0.7 all-gather.9.cloned.1.call-update
  7.9 0.0 all-gather.7.cloned.1.call-start
  8.0 1.2 fusion.27
  9.2 0.0 copy-done
  9.2 0.9 convolution_convert_fusion
  10.0 0.0 all-gather.7.cloned.1.call-update
  10.1 0.7 convert_element_type.64
  10.7 0.0 copy-done.3
  10.7 0.6 reduce-window.6
  11.3 0.2 slice_reduce_fusion
  11.6 0.1 fusion.31
  11.7 2.0 scatter_custom_fusion
  13.7 7.3 %all-to-all-start = ((f32[8,1,128]{2,1,0:T(1,128)}), f32[8,1,128]{2,1,0:T(1,128)S(1)}, u32[]{:S(2)}, u32[]{:S(2)}) async-start(f32[8,1,128]{2,1,0:T(1,128)} %bitcast.13), calls=%async_computation | async-start | bytes 8192 | tf_op jit(solution)/shard_map/all_to_all | solution.py:81
  20.9 0.0 copy-done.5
  21.0 21.1 %all-gather.3 = f32[8,1,256]{2,1,0:T(1,128)S(1)} all-gather(f32[1,1,256]{2,1,0:T(1,128)S(1)} %bitcast.67), channel_id=1, replica_groups=mesh['rows'=8,'grp'=4] {'rows'}, dimensions={0}, use_global_device_ids=true | all-gather | bytes 9216 | tf_op jit(solution)/shard_map/all_gather | solution.py:48
  42.1 0.0 copy-done.4
  42.1 16.3 %all-gather.1 = f32[1,2048]{1,0:T(1,128)S(1)} all-gather(f32[1,256]{1,0:T(1,128)S(1)} %copy-done.4), channel_id=3, replica_groups=mesh['rows'=8,'grp'=4] {'rows'}, dimensions={1}, use_global_device_ids=true | all-gather | bytes 9216 | tf_op jit(solution)/shard_map/all_gather | solution.py:50
  58.4 1.9 fusion.37
  60.3 0.4 exponential_reduce_fusion
  60.7 18.3 %all-gather.2 = f32[8,1,256]{2,1,0:T(1,128)S(1)} all-gather(f32[1,1,256]{2,1,0:T(1,128)S(1)} %bitcast.66), channel_id=1, replica_groups=mesh['rows'=8,'grp'=4] {'rows'}, dimensions={0}, use_global_device_ids=true | all-gather | bytes 9216 | tf_op jit(solution)/shard_map/all_gather | solution.py:49
  79.1 16.1 %all-gather.7.cloned.1.call-done = bf16[2048,256]{1,0:T(8,128)(2,1)} async-done(((bf16[256,256]{1,0:T(8,128)(2,1)}), bf16[2048,256]{1,0:T(8,128)(2,1)}) %all-gather.7.cloned.1.call-update) | async-done | bytes 1048592 | tf_op jit(solution)/shard_map/all_gather | solution.py:46
  95.2 3.9 %fusion.6 = f32[256,256]{1,0:T(8,128)} fusion(bf16[2048,256]{1,0:T(8,128)(2,1)} %all-gather.7.cloned.1.call-done, s32[256]{0:T(256)S(1)} %iota_add_fusion, f32[2048]{0:T(1024)S(1)} %bitcast.64, f32[2048]{0:T(1024)S(1)} %bitcast.63, s32[2048]{0:T(1024)S(1)} %bitcast.65, bf16[1,256,256]{2,1,0:T(8,128)(2,1)S(1)} %copy-done.2), kind=kOutput, calls=%fused_computation.13 | convolution fusion | flops 540016640 | bytes 1467392 | tf_op jit(solution)/shard_map/dot_general | solution.py:10
  99.1 2.9 scatter_custom_fusion.1
  102.0 0.0 all-to-all-done
  102.0 4.4 %all-to-all-start.1 = ((f32[8,128,256]{2,1,0:T(8,128)}), f32[8,128,256]{2,1,0:T(8,128)}, u32[]{:S(2)}, u32[]{:S(2)}) async-start(f32[8,128,256]{2,1,0:T(8,128)} %bitcast.22), calls=%async_computation.1 | async-start | bytes 2097152 | tf_op jit(solution)/shard_map/all_to_all | solution.py:80
  106.3 0.0 all-reduce.3.cloned.1.call-start
  106.4 0.0 copy-done.1
  106.4 0.0 copy-done.6
  106.4 0.8 convolution_convert_fusion.1
  107.2 0.0 copy-start.7
  107.2 0.6 copy-done.7
  107.8 1.0 fusion.36
  108.8 2.1 convolution_bitcast_fusion
  110.9 0.0 all-reduce.3.cloned.1.call-update
  111.0 0.0 reduce-scatter.4.cloned.1.call-start
  111.0 20.8 %all-to-all-done.1 = f32[8,128,256]{2,1,0:T(8,128)} async-done(((f32[8,128,256]{2,1,0:T(8,128)}), f32[8,128,256]{2,1,0:T(8,128)}, u32[]{:S(2)}, u32[]{:S(2)}) %all-to-all-start.1) | async-done | bytes 1048608 | tf_op jit(solution)/shard_map/all_to_all | solution.py:80
  131.8 8.7 %scatter_custom_fusion.2 = f32[4096,256]{1,0:T(8,128)} fusion(s32[1024]{0:T(1024)S(1)} %bitcast.68, f32[1024,256]{1,0:T(8,128)} %bitcast.23, f32[]{:T(128)} %constant.13.clone.1), kind=kCustom, calls=%fused_computation.8 | custom fusion | flops 262144 | bytes 4194816 | tf_op jit(solution)/shard_map/scatter-add | solution.py:90
  140.5 5.7 %copy.16 = f32[4096,256]{0,1:T(8,128)} copy(f32[4096,256]{1,0:T(8,128)} %scatter_custom_fusion.2) | data formatting | bytes 8388608
  146.1 0.0 reduce-scatter.4.cloned.1.call-update
  146.2 100.4 %all-reduce.3.cloned.1.call-done = (f32[256,256]{0,1:T(8,128)}, f32[256,256]{1,0:T(8,128)}) async-done(((f32[256,256]{0,1:T(8,128)}, f32[256,256]{1,0:T(8,128)}), (f32[256,256]{0,1:T(8,128)}, f32[256,256]{1,0:T(8,128)})) %all-reduce.3.cloned.1.call-update) | async-done | bytes 524304 | tf_op jit(solution)/shard_map/psum | solution.py:66
  246.5 1.8 copy.14
  248.3 44.8 %reduce-scatter.4.cloned.1.call-done = f32[64,4096]{1,0:T(8,128)} async-done(((f32[256,4096]{1,0:T(8,128)}), f32[64,4096]{1,0:T(8,128)}) %reduce-scatter.4.cloned.1.call-update) | async-done | bytes 1048592
  293.1 1.7 copy.20
  (14 shorter events, 0.1 us)
Async XLA Ops:
  7.2 2.0 copy-start
  7.2 3.6 %copy-start.3 = (s32[1,256,1]{1,2,0:T(1,128)S(1)}, s32[1,256,1]{1,2,0:T(1,128)}, u32[]{:S(2)}) copy-start(s32[1,256,1]{1,2,0:T(1,128)} %param.14) | copy-start | bytes 3076
  7.2 13.8 %copy-start.5 = (s32[1,256]{1,0:T(1,128)S(1)}, s32[1,256]{1,0:T(1,128)}, u32[]{:S(2)}) copy-start(s32[1,256]{1,0:T(1,128)} %param.13) | copy-start | bytes 3076
  7.2 34.9 %copy-start.4 = (f32[1,256]{1,0:T(1,128)S(1)}, f32[1,256]{1,0:T(1,128)}, u32[]{:S(2)}) copy-start(f32[1,256]{1,0:T(1,128)} %param.12) | copy-start | bytes 3076
  7.2 51.2 %all-gather.9.cloned.1.call-start = ((), (), s32[]{:S(2)}) async-start(), calls=%async_computation.4 | async-start | bytes 1179648 | tf_op jit(solution)/shard_map/all_gather | solution.py:37
  7.9 87.2 %all-gather.7.cloned.1.call-start = ((), (), s32[]{:S(2)}) async-start(), calls=%async_computation.3 | async-start | bytes 1179648 | tf_op jit(solution)/shard_map/all_gather | solution.py:46
  13.7 88.3 %all-to-all-start = ((f32[8,1,128]{2,1,0:T(1,128)}), f32[8,1,128]{2,1,0:T(1,128)S(1)}, u32[]{:S(2)}, u32[]{:S(2)}) async-start(f32[8,1,128]{2,1,0:T(1,128)} %bitcast.13), calls=%async_computation | async-start | bytes 8192 | tf_op jit(solution)/shard_map/all_to_all | solution.py:81
  58.4 36.8 %copy-start.2 = (bf16[1,256,256]{2,1,0:T(8,128)(2,1)S(1)}, bf16[1,256,256]{2,1,0:T(8,128)(2,1)}, u32[]{:S(2)}) copy-start(bf16[1,256,256]{2,1,0:T(8,128)(2,1)} %param.11) | copy-start | bytes 393220
  99.1 7.3 %copy-start.1 = (bf16[1,2048,256]{2,1,0:T(8,128)(2,1)S(1)}, bf16[1,2048,256]{2,1,0:T(8,128)(2,1)}, u32[]{:S(2)}) copy-start(bf16[1,2048,256]{2,1,0:T(8,128)(2,1)} %all-gather.9.cloned.1.call-done) | copy-start | bytes 3145732
  102.0 4.4 %copy-start.6 = (s32[1,256]{1,0:T(1,128)S(1)}, s32[1,256]{1,0:T(1,128)}, u32[]{:S(2)}) copy-start(s32[1,256]{1,0:T(1,128)} %param.13) | copy-start | bytes 3076
  102.0 29.8 %all-to-all-start.1 = ((f32[8,128,256]{2,1,0:T(8,128)}), f32[8,128,256]{2,1,0:T(8,128)}, u32[]{:S(2)}, u32[]{:S(2)}) async-start(f32[8,128,256]{2,1,0:T(8,128)} %bitcast.22), calls=%async_computation.1 | async-start | bytes 2097152 | tf_op jit(solution)/shard_map/all_to_all | solution.py:80
  106.3 140.2 %all-reduce.3.cloned.1.call-start = ((), (), s32[]{:S(2)}) async-start(), calls=%async_computation.6 | async-start | bytes 1048576 | tf_op jit(solution)/shard_map/psum | solution.py:66
  107.2 0.6 copy-start.7
  111.0 182.1 %reduce-scatter.4.cloned.1.call-start = ((), (), s32[]{:S(2)}) async-start(), calls=%async_computation.5 | async-start | bytes 5242880
Sparse Core Ops, SparseCore 0:
  10.1 43.2 all-gather.8
  56.1 38.9 all-gather.6
  113.2 133.2 all-reduce.2
  249.5 43.5 reduce-scatter.3
where the time goes:
time: 302 us; the launch traced here: 301 us
  waiting for transfers between devices  183 us (61%)
  blocking collectives  55.7 us (18%)
  local copies, waits for them, and re-layouts  14.9 us (5%)
  between operations  13.9 us (5%)
  starting transfers between devices  11.8 us (4%)
  matrix products  11.7 us (4%)
  other arithmetic  10.6 us (4%)
    psum x1, waiting for transfers between devices, body(): grad_first, grad_second = lax.psum((d_first, d_second), ('rows', 'grp'))  100 us
    unnamed x5, waiting for transfers between devices  45.5 us
    all_gather x1, blocking collectives, body(): lax.all_gather(targets.astype(jnp.float32), 'rows', axis=0, tiled=True)  21.1 us
    all_to_all x1, waiting for transfers between devices, body(): lax.all_to_all(send_grad, 'rows', split_axis=0, concat_axis=0, tiled=True)  20.8 us
    all_gather x1, blocking collectives, body(): lax.all_gather(log_total[:, 0], 'rows', axis=0, tiled=True)  18.3 us
    all_gather x1, blocking collectives, body(): lax.all_gather(weights, 'rows', axis=0, tiled=True)  16.3 us
    all_gather x1, waiting for transfers between devices, body(): everyone = lax.all_gather(user_vecs, 'rows', axis=0, tiled=True)  16.1 us
    unnamed x19, local copies, waits for them, and re-layouts  9.79 us
  transfers between devices with their start and end apart: 6, of which 4 were waited for; matrix products, arithmetic and copies ran while one was open for 12% of the time, Pallas kernels for 0%

commit v1 on v0

v1 whole, which is shorter than its diff:
```python
import functools
import jax
import jax.numpy as jnp
from jax import lax
from jax.experimental import pallas as pl
from jax.experimental.pallas import tpu as pltpu
from jax.sharding import PartitionSpec as P

ITEMS_DEV = 4096
F32 = jnp.float32
BF16 = jnp.bfloat16
MESH = pl.DeviceIdType.MESH


def mm(left, right, ld, rd):
    return lax.dot_general(left, right, (((ld,), (rd,)), ((), ())), preferred_element_type=F32)


def kernel(
    n, ng, lows,
    feat, w1, w2, items, stats_in,
    table, g_first, g_second,
    items_g, users_g, gat, sc, pre_buf, hid_buf, gu, gi, gt, acc,
    stats_out, stats_g, ids_in, ids_g,
    dgrad, s1_recv, s2_send, s2_recv, s3_send, s3_recv, q_buf, fin,
    ring_s, ring_r, st_s, st_r, id_s, id_r, gt_s, gt_r,
    d1_s, d1_r, d2_s, d2_r, d3_s, d3_r, d4_s, d4_r,
):
    me = lax.axis_index("rows")
    grp = lax.axis_index("grp")
    m = items.shape[0]
    half = m // 2
    full = n // 2 - 1
    cols = table.shape[0]
    span = ITEMS_DEV // lows

    def at_pos(p):
        p = lax.rem(p + 2 * n, n)
        return jnp.where(p < n // 2, 2 * p, 2 * (n - 1 - p) + 1)

    odd = lax.rem(me, 2)
    pos = jnp.where(odd == 0, me // 2, n - 1 - me // 2)
    right, left = at_pos(pos + 1), at_pos(pos - 1)

    def row_peer(k):
        return lax.rem(me + k, n)

    def grp_peer(k):
        return lax.rem(grp + k, ng)

    def remote(src, dst, ss, rs, rows=None, grps=None):
        return pltpu.make_async_remote_copy(
            src_ref=src, dst_ref=dst, send_sem=ss, recv_sem=rs,
            device_id=(me if rows is None else rows, grp if grps is None else grps),
            device_id_type=MESH,
        )

    def hop(which, buf, h, d, c, first=None):
        origin = at_pos(pos - h) if d == 0 else at_pos(pos + h)
        size = buf.shape[1] // 2
        dst = buf.at[origin, pl.ds(c * size, size)]
        src = dst if first is None else first.at[pl.ds(c * size, size)]
        return remote(
            src, dst, ring_s.at[which, d, h, c], ring_r.at[which, d, h, c],
            rows=right if d == 0 else left,
        )

    def arrive(which, buf, h, d, c):
        origin = at_pos(pos - h - 1) if d == 0 else at_pos(pos + h + 1)
        size = buf.shape[1] // 2
        dst = buf.at[origin, pl.ds(c * size, size)]
        remote(
            dst, dst, ring_s.at[which, d, h, c], ring_r.at[which, d, h, c],
            rows=right if d == 0 else left,
        ).wait_recv()
        return origin

    def ring_start(which, buf, first=None):
        for c in range(2):
            for d in range(2):
                if full > 0 or c == d:
                    hop(which, buf, 0, d, c, first).start()

    def ring_full(which, buf, h):
        for c in range(2):
            for d in range(2):
                arrive(which, buf, h, d, c)
                hop(which, buf, h + 1, d, c).start()

    def ring_turn(which, buf, h):
        for d in range(2):
            arrive(which, buf, h, d, d)
            hop(which, buf, h + 1, d, d).start()
        for d in range(2):
            arrive(which, buf, h, d, 1 - d)

    def ring_end(which, buf):
        for d in range(2):
            arrive(which, buf, full, d, d)

    def ring_sent(which, buf, first=None):
        for d in range(2):
            for c in range(2):
                for h in range(full + 1):
                    if h < full or c == d:
                        hop(which, buf, h, d, c, first if h == 0 else None).wait_send()

    def behind(h):
        return at_pos(pos - h - 1), at_pos(pos + h + 1)

    far = at_pos(pos + n // 2)

    barrier = pltpu.get_barrier_semaphore()
    for k in range(1, n):
        pl.semaphore_signal(barrier, inc=1, device_id=(row_peer(k), grp), device_id_type=MESH)
    for k in range(1, ng):
        pl.semaphore_signal(barrier, inc=1, device_id=(me, grp_peer(k)), device_id_type=MESH)

    pre = mm(feat[...], w1[...], 1, 0)
    pre_buf[...] = pre
    hidden = (pre * jax.nn.sigmoid(pre)).astype(BF16)
    hid_buf[...] = hidden
    own_users = mm(hidden, w2[...], 1, 0).astype(BF16)
    users_g[me] = own_users
    items_g[me] = items[...]
    acc[...] = jnp.zeros_like(acc)

    pl.semaphore_wait(barrier, n - 1 + ng - 1)
    ring_start(0, items_g, items)

    def id_copy(k):
        return remote(stats_in, ids_in.at[grp], id_s.at[k - 1], id_r.at[k - 1], grps=grp_peer(k))

    for k in range(1, ng):
        id_copy(k).start()

    def score(b, top):
        s = mm(items_g[b], users_g[me], 1, 1)
        sc[b] = s
        return jnp.maximum(top, jnp.max(s, axis=0, keepdims=True))

    top = score(me, jnp.full((1, m), -jnp.inf, F32))

    def step_items(h, top):
        ring_full(0, items_g, h)
        for b in behind(h):
            top = score(b, top)
        return top

    if full > 0:
        top = lax.fori_loop(0, full - 1, step_items, top)
        ring_turn(0, items_g, full - 1)
    ring_start(1, users_g)
    if full > 0:
        for b in behind(full - 1):
            top = score(b, top)
    ring_end(0, items_g)
    top = score(far, top)

    weight = stats_in[1:2, :]
    target = stats_in[2:3, :].astype(jnp.int32)

    total = lax.fori_loop(
        0, n, lambda b, t: t + jnp.sum(jnp.exp(sc[b] - top), axis=0, keepdims=True),
        jnp.zeros((1, m), F32),
    )
    log_total = top + jnp.log(total)

    ids_in[grp] = stats_in[...]
    for k in range(1, ng):
        src = lax.rem(grp + ng - k, ng)
        remote(
            stats_in, ids_in.at[src], id_s.at[k - 1], id_r.at[k - 1], grps=grp_peer(k)
        ).wait_recv()
    stats_out[0:1, :] = log_total
    stats_out[1:2, :] = weight
    stats_out[2:3, :] = stats_in[2:3, :]
    for q in range(ng):
        stats_out[3 + q : 4 + q, :] = ids_in[q, 3:4, :]
    for q in range(3 + ng, stats_out.shape[0]):
        stats_out[q : q + 1, :] = jnp.zeros((1, m), F32)

    def stat_copy(k, slot):
        return remote(stats_out, stats_g.at[slot], st_s.at[k - 1], st_r.at[k - 1], rows=row_peer(k))

    for k in range(1, n):
        stat_copy(k, me).start()
    stats_g[me] = stats_out[...]
    if full > 1:
        ring_full(1, users_g, 0)

    gu[...] = jnp.zeros_like(gu)

    def back_user(b, carry):
        rows_at = b * m + lax.broadcasted_iota(jnp.int32, (m, m), 0)
        hit = (rows_at == target).astype(F32)
        ds = (weight * (jnp.exp(sc[b] - log_total) - hit)).astype(BF16)
        gu[...] += mm(ds, items_g[b], 0, 0)
        return carry

    lax.fori_loop(0, n, back_user, 0)
    grad_user = gu[...].astype(BF16)
    back = mm(grad_user, w2[...], 1, 1)
    pre = pre_buf[...]
    sig = jax.nn.sigmoid(pre)
    grad_pre = (back * sig * (1.0 + pre * (1.0 - sig))).astype(BF16)
    dh = w1.shape[0]
    dgrad[0:dh, :] = mm(feat[...], grad_pre, 0, 0)
    dgrad[dh:, :] = mm(hid_buf[...], grad_user, 0, 0)
    quarter = dgrad.shape[0] // ng

    def d1_copy(k):
        return remote(
            dgrad.at[pl.ds(pl.multiple_of(grp_peer(k) * quarter, quarter), quarter)],
            s1_recv.at[k - 1], d1_s.at[k - 1], d1_r.at[k - 1], grps=grp_peer(k),
        )

    for k in range(1, ng):
        d1_copy(k).start()

    for k in range(1, n):
        stat_copy(k, lax.rem(me + n - k, n)).wait_recv()
    own_rows = me * m + lax.broadcasted_iota(jnp.int32, (m, m), 0)
    gi[...] = jnp.zeros_like(gi)

    def back_item(b):
        st = stats_g[b]
        s = mm(items[...], users_g[b], 1, 1)
        hit = (own_rows == st[2:3, :].astype(jnp.int32)).astype(F32)
        ds = (st[1:2, :] * (jnp.exp(s - st[0:1, :]) - hit)).astype(BF16)
        gi[...] += mm(ds, users_g[b], 1, 0)

    back_item(me)
    if full > 1:
        for b in behind(0):
            back_item(b)

    def step_users(h, carry):
        ring_full(1, users_g, h)
        for b in behind(h):
            back_item(b)
        return carry

    if full > 0:
        if full > 2:
            lax.fori_loop(1, full - 1, step_users, 0)
        ring_turn(1, users_g, full - 1)
        for b in behind(full - 1):
            back_item(b)

    piece = quarter // n
    for k in range(1, ng):
        d1_copy(k).wait_recv()
    part = dgrad[pl.ds(pl.multiple_of(grp * quarter, quarter), quarter), :]
    for k in range(1, ng):
        part = part + s1_recv[k - 1]
    for q in range(n):
        s2_send[q] = part[q * piece : (q + 1) * piece, :]

    def d2_copy(k):
        return remote(
            s2_send.at[row_peer(k)], s2_recv.at[k - 1], d2_s.at[k - 1], d2_r.at[k - 1],
            rows=row_peer(k),
        )

    for k in range(1, n):
        d2_copy(k).start()

    ring_end(1, users_g)
    back_item(far)
    turned = jnp.transpose(gi[...]).astype(BF16)
    for q in range(ng):
        gt[q] = turned[q * cols : (q + 1) * cols, :]

    def gt_copy(k, slot):
        return remote(
            gt.at[grp_peer(k)], gat.at[me, slot], gt_s.at[k - 1], gt_r.at[k - 1], grps=grp_peer(k)
        )

    for k in range(1, ng):
        gt_copy(k, grp).start()
    gat[me, grp] = gt[grp]

    for k in range(1, n):
        d2_copy(k).wait_recv()
    one = s2_send[me]
    for k in range(1, n):
        one = one + s2_recv[k - 1]
    s3_send[...] = one
    s3_recv[me] = one

    for k in range(1, ng):
        gt_copy(k, lax.rem(grp + ng - k, ng)).wait_recv()
    ring_start(2, gat)

    def d3_copy(k, slot):
        return remote(s3_send, s3_recv.at[slot], d3_s.at[k - 1], d3_r.at[k - 1], rows=row_peer(k))

    for k in range(1, n):
        d3_copy(k, me).start()

    def place(b):
        ids = stats_g[b, 3 : 3 + ng, :].astype(jnp.int32) - me * ITEMS_DEV
        for q in range(ng):
            own = ids[q : q + 1, :]
            own = jnp.where((own >= 0) & (own < ITEMS_DEV), own, -1)
            low = own // span
            high = jnp.where(own < 0, -1, own - low * span)
            pick = (lax.broadcasted_iota(jnp.int32, (span, m), 0) == high).astype(F32).astype(BF16)
            values = gat[b, q]
            zero = jnp.zeros_like(values)
            lifted = jnp.concatenate(
                [
                    jnp.where(jnp.broadcast_to(low, values.shape) == v, values, zero)
                    for v in range(lows)
                ],
                axis=0,
            )
            acc[...] += mm(lifted, pick, 1, 1)

    place(me)

    def step_table(h, carry):
        ring_full(2, gat, h)
        for b in behind(h):
            place(b)
        return carry

    if full > 0:
        lax.fori_loop(0, full - 1, step_table, 0)
        ring_turn(2, gat, full - 1)

    for k in range(1, n):
        d3_copy(k, lax.rem(me + n - k, n)).wait_recv()
    q_buf[...] = jnp.concatenate([s3_recv[q] for q in range(n)], axis=0).astype(BF16)
    fin[grp] = q_buf[...]

    def d4_copy(k, slot):
        return remote(q_buf, fin.at[slot], d4_s.at[k - 1], d4_r.at[k - 1], grps=grp_peer(k))

    for k in range(1, ng):
        d4_copy(k, grp).start()

    if full > 0:
        for b in behind(full - 1):
            place(b)
    ring_end(2, gat)
    place(far)
    for v in range(lows):
        table[:, v * span : (v + 1) * span] = acc[v * cols : (v + 1) * cols, :]

    for k in range(1, ng):
        d4_copy(k, lax.rem(grp + ng - k, ng)).wait_recv()
    for q in range(ng):
        first = q * quarter
        out, base = (g_first, first) if first < dh else (g_second, first - dh)
        out[base : base + quarter, :] = fin[q].astype(F32)

    ring_sent(0, items_g, items)
    ring_sent(1, users_g)
    ring_sent(2, gat)
    for k in range(1, n):
        stat_copy(k, me).wait_send()
        d2_copy(k).wait_send()
        d3_copy(k, me).wait_send()
    for k in range(1, ng):
        id_copy(k).wait_send()
        d1_copy(k).wait_send()
        gt_copy(k, grp).wait_send()
        d4_copy(k, grp).wait_send()


def body(
    n, ng,
    user_features, w_first, w_second, item_embed, example_weight, positive, item_owner, item_row
):
    m, d = item_embed.shape[1], item_embed.shape[2]
    dh = w_first.shape[0]
    cols = d // ng
    lows = 8
    span = ITEMS_DEV // lows
    ids = item_owner[:, :, 0] * ITEMS_DEV + item_row
    stats_in = jnp.concatenate(
        [
            jnp.zeros((1, m), F32), example_weight, positive.astype(F32), ids.astype(F32),
            jnp.zeros((4, m), F32),
        ],
        axis=0,
    )
    srows = -(-(3 + ng) // 8) * 8
    quarter = 2 * dh // ng
    piece = quarter // n
    hops = n // 2
    vmem = pl.BlockSpec(memory_space=pltpu.VMEM)
    sem = pltpu.SemaphoreType.DMA
    table, g_first, g_second = pl.pallas_call(
        functools.partial(kernel, n, ng, lows),
        out_shape=(
            jax.ShapeDtypeStruct((cols, ITEMS_DEV), F32),
            jax.ShapeDtypeStruct(w_first.shape, F32),
            jax.ShapeDtypeStruct(w_second.shape, F32),
        ),
        in_specs=[vmem] * 5,
        out_specs=(vmem,) * 3,
        scratch_shapes=[
            pltpu.VMEM((n, m, d), BF16),
            pltpu.VMEM((n, m, d), BF16),
            pltpu.VMEM((n, ng, cols, m), BF16),
            pltpu.VMEM((n, m, m), F32),
            pltpu.VMEM((m, dh), F32),
            pltpu.VMEM((m, dh), BF16),
            pltpu.VMEM((m, d), F32),
            pltpu.VMEM((m, d), F32),
            pltpu.VMEM((ng, cols, m), BF16),
            pltpu.VMEM((lows * cols, span), F32),
            pltpu.VMEM((srows, m), F32),
            pltpu.VMEM((n, srows, m), F32),
            pltpu.VMEM((ng, 8, m), F32),
            pltpu.VMEM((8, m), F32),
            pltpu.VMEM((2 * dh, d), F32),
            pltpu.VMEM((ng - 1, quarter, d), F32),
            pltpu.VMEM((n, piece, d), F32),
            pltpu.VMEM((n - 1, piece, d), F32),
            pltpu.VMEM((piece, d), F32),
            pltpu.VMEM((n, piece, d), F32),
            pltpu.VMEM((quarter, d), BF16),
            pltpu.VMEM((ng, quarter, d), BF16),
            sem((3, 2, hops, 2)), sem((3, 2, hops, 2)),
            sem((n - 1,)), sem((n - 1,)),
            sem((ng - 1,)), sem((ng - 1,)),
            sem((ng - 1,)), sem((ng - 1,)),
            sem((ng - 1,)), sem((ng - 1,)),
            sem((n - 1,)), sem((n - 1,)),
            sem((n - 1,)), sem((n - 1,)),
            sem((ng - 1,)), sem((ng - 1,)),
        ],
        compiler_params=pltpu.CompilerParams(
            collective_id=0, has_side_effects=True, vmem_limit_bytes=60 * 1024 * 1024
        ),
    )(user_features[0], w_first, w_second, item_embed[0], stats_in)
    return g_first, g_second, jnp.transpose(table)


def solution(mesh):
    placed = (
        P("grp", "rows", None),
        P(),
        P(),
        P("grp", "rows", None),
        P("grp", "rows"),
        P("grp", "rows"),
        P("grp", "rows", None),
        P("grp", "rows"),
    )
    return jax.shard_map(
        functools.partial(body, mesh.shape["rows"], mesh.shape["grp"]),
        mesh=mesh, in_specs=placed, out_specs=(P(), P(), P("rows", "grp")), check_vma=False
    )
```

time: 302 us -> 70.4 us (0.23)
  waiting for transfers between devices: 183 us -> 0 us
  Pallas kernels: 0 us -> 62.4 us
  blocking collectives: 55.7 us -> 0 us
  between operations: 13.9 us -> 0.67 us
  starting transfers between devices: 11.8 us -> 0 us
  matrix products: 11.7 us -> 0 us
  other arithmetic: 10.6 us -> 0.01 us
  local copies, waits for them, and re-layouts: 14.9 us -> 7.05 us
    psum x1 -> x0, waiting for transfers between devices: 100 us -> none  [body(): grad_first, grad_second = lax.psum((d_first, d_second), ('rows', 'grp'))]
    pallas_call x0 -> x1, Pallas kernels: none -> 62.4 us  [body(): pl.pallas_call(functools.partial(kernel, n, ng, lows), out_shape=(jax.Sha...]
    all_gather x3 -> x0, blocking collectives: 55.7 us -> none  [the longest x1 21.1 us: body(): lax.all_gather(targets.astype(jnp.float32), 'rows', axis=0, tiled=True)]
    unnamed x5 -> x0, waiting for transfers between devices: 45.5 us -> none
    all_to_all x2 -> x0, waiting for transfers between devices: 20.8 us -> none  [the longest x1 20.8 us: body(): lax.all_to_all(send_grad, 'rows', split_axis=0, concat_axis=0, tiled=True)]
    all_gather x2 -> x0, waiting for transfers between devices: 16.1 us -> none  [the longest x1 16.1 us: body(): everyone = lax.all_gather(user_vecs, 'rows', axis=0, tiled=True)]
    dot_general x7 -> x0, matrix products: 11.7 us -> none  [the longest x3 7.02 us: contract_first(): lax.dot_general(left, right, (((0,), (0,)), ((), ())), preferred_element_...]
    all_to_all x2 -> x0, starting transfers between devices: 11.7 us -> none  [the longest x1 7.28 us: body(): lax.all_to_all(send_rows.reshape(peers, capacity), 'rows', split_axis=0,...]
  transfers between devices with their start and end apart: 6 -> 0, of which waited for: 4 -> 0; matrix products, arithmetic and copies ran while one was open for 12% -> 0% of each run, Pallas kernels for 0% -> 0%
where the time goes in v1:
time: 70.4 us; the launch traced here: 70.1 us
  Pallas kernels  62.4 us (89%)
  local copies, waits for them, and re-layouts  7.05 us (10%)
    pallas_call x1, Pallas kernels, body(): pl.pallas_call(functools.partial(kernel, n, ng, lows), out_shape=(jax.Sha...  62.4 us
    unnamed x13, local copies, waits for them, and re-layouts  6.43 us

profile of v1, /device:TPU:0, one launch (start us, length us, event | category | flops | bytes accessed | tf_op | source)
XLA Modules:
  0.0 70.1 jit_solution(9314211232736746062)
XLA Ops:
  0.6 0.0 copy-start.4
  0.6 0.7 copy-done.4
  1.3 0.0 copy-start.1
  1.3 0.0 copy-start.2
  1.3 0.7 copy-done.1
  2.0 0.0 copy-done.2
  2.0 0.0 copy-start.3
  2.0 0.7 copy-done.3
  2.7 0.6 concatenate.3.stats_in
  3.3 62.4 %shard_map.103 = (f32[64,4096]{1,0:T(8,128)}, f32[256,256]{1,0:T(8,128)}, f32[256,256]{1,0:T(8,128)}) custom-call(bf16[256,256]{1,0:T(8,128)(2,1)} %bitcast.8, bf16[256,256]{1,0:T(8,128)(2,1)} %w1.1, bf16[256,256]{1,0:T(8,128)(2,1)} %w2.1, bf16[256,256]{1,0:T(8,128)(2,1)} %bitcast.9, f32[8,256]{1,0:T(8,128)} %concatenate.3.stats_in), custom_call_target="tpu_custom_call" | custom-call | tf_op jit(solution)/shard_map/pallas_call | solution.py:396
  65.7 0.0 copy-start
  65.7 1.8 %copy.14 = f32[256,256]{1,0:T(8,128)} copy(f32[256,256]{1,0:T(8,128)} %get-tuple-element.12) | data formatting | bytes 524288
  67.5 1.7 %copy.15 = f32[256,256]{1,0:T(8,128)} copy(f32[256,256]{1,0:T(8,128)} %get-tuple-element.13) | data formatting | bytes 524288
  69.2 0.0 copy-done
  69.2 1.0 %copy.16 = f32[4096,64]{0,1:T(8,128)} copy(f32[4096,64]{0,1:T(8,128)S(1)} %bitcast.7) | data formatting | bytes 2097152
  (4 shorter events, 0.0 us)
Async XLA Ops:
  0.6 0.7 copy-start.4
  1.3 0.7 copy-start.1
  1.3 0.7 copy-start.2
  2.0 0.7 copy-start.3
  65.7 3.4 %copy-start = (f32[64,4096]{1,0:T(8,128)S(1)}, f32[64,4096]{1,0:T(8,128)}, u32[]{:S(2)}) copy-start(f32[64,4096]{1,0:T(8,128)} %get-tuple-element.8) | copy-start | bytes 3145732

commit v2 on v1

--- a/solution.py
+++ b/solution.py
@@ -10,6 +10,7 @@
 F32 = jnp.float32
 BF16 = jnp.bfloat16
 MESH = pl.DeviceIdType.MESH
+CHUNKS = 4
 
 
 def mm(left, right, ld, rd):
@@ -18,10 +19,10 @@
 
 def kernel(
     n, ng, lows,
-    feat, w1, w2, items, stats_in,
-    table, g_first, g_second,
+    feat, w1, w2, items, weight_in, target_in, owner_in, row_in,
+    table, g_both,
     items_g, users_g, gat, sc, pre_buf, hid_buf, gu, gi, gt, acc,
-    stats_out, stats_g, ids_in, ids_g,
+    stats_out, stats_g, ids_in, stats_in,
     dgrad, s1_recv, s2_send, s2_recv, s3_send, s3_recv, q_buf, fin,
     ring_s, ring_r, st_s, st_r, id_s, id_r, gt_s, gt_r,
     d1_s, d1_r, d2_s, d2_r, d3_s, d3_r, d4_s, d4_r,
@@ -29,7 +30,7 @@
     me = lax.axis_index("rows")
     grp = lax.axis_index("grp")
     m = items.shape[0]
-    half = m // 2
+    lasts = (range(CHUNKS // 2), range(CHUNKS // 2, CHUNKS))
     full = n // 2 - 1
     cols = table.shape[0]
     span = ITEMS_DEV // lows
@@ -57,7 +58,7 @@
 
     def hop(which, buf, h, d, c, first=None):
         origin = at_pos(pos - h) if d == 0 else at_pos(pos + h)
-        size = buf.shape[1] // 2
+        size = buf.shape[1] // CHUNKS
         dst = buf.at[origin, pl.ds(c * size, size)]
         src = dst if first is None else first.at[pl.ds(c * size, size)]
         return remote(
@@ -67,7 +68,7 @@
 
     def arrive(which, buf, h, d, c):
         origin = at_pos(pos - h - 1) if d == 0 else at_pos(pos + h + 1)
-        size = buf.shape[1] // 2
+        size = buf.shape[1] // CHUNKS
         dst = buf.at[origin, pl.ds(c * size, size)]
         remote(
             dst, dst, ring_s.at[which, d, h, c], ring_r.at[which, d, h, c],
@@ -76,33 +77,34 @@
         return origin
 
     def ring_start(which, buf, first=None):
-        for c in range(2):
+        for c in range(CHUNKS):
             for d in range(2):
-                if full > 0 or c == d:
+                if full > 0 or c in lasts[d]:
                     hop(which, buf, 0, d, c, first).start()
 
     def ring_full(which, buf, h):
-        for c in range(2):
+        for c in range(CHUNKS):
             for d in range(2):
                 arrive(which, buf, h, d, c)
                 hop(which, buf, h + 1, d, c).start()
 
     def ring_turn(which, buf, h):
-        for d in range(2):
-            arrive(which, buf, h, d, d)
-            hop(which, buf, h + 1, d, d).start()
-        for d in range(2):
-            arrive(which, buf, h, d, 1 - d)
+        for c in range(CHUNKS):
+            for d in range(2):
+                arrive(which, buf, h, d, c)
+                if c in lasts[d]:
+                    hop(which, buf, h + 1, d, c).start()
 
     def ring_end(which, buf):
         for d in range(2):
-            arrive(which, buf, full, d, d)
+            for c in lasts[d]:
+                arrive(which, buf, full, d, c)
 
     def ring_sent(which, buf, first=None):
         for d in range(2):
-            for c in range(2):
+            for c in range(CHUNKS):
                 for h in range(full + 1):
-                    if h < full or c == d:
+                    if h < full or c in lasts[d]:
                         hop(which, buf, h, d, c, first if h == 0 else None).wait_send()
 
     def behind(h):
@@ -124,9 +126,14 @@
     users_g[me] = own_users
     items_g[me] = items[...]
     acc[...] = jnp.zeros_like(acc)
+    stats_in[...] = jnp.zeros_like(stats_in)
+    stats_in[1:2, :] = weight_in[...]
+    stats_in[2:3, :] = target_in[...].astype(F32)
+    stats_in[3:4, :] = (owner_in[...] * ITEMS_DEV + row_in[...]).astype(F32)
 
     pl.semaphore_wait(barrier, n - 1 + ng - 1)
     ring_start(0, items_g, items)
+    ring_start(1, users_g)
 
     def id_copy(k):
         return remote(stats_in, ids_in.at[grp], id_s.at[k - 1], id_r.at[k - 1], grps=grp_peer(k))
@@ -149,16 +156,18 @@
 
     if full > 0:
         top = lax.fori_loop(0, full - 1, step_items, top)
+    if full > 0:
         ring_turn(0, items_g, full - 1)
-    ring_start(1, users_g)
     if full > 0:
         for b in behind(full - 1):
             top = score(b, top)
     ring_end(0, items_g)
+    if full > 1:
+        ring_full(1, users_g, 0)
     top = score(far, top)
 
     weight = stats_in[1:2, :]
-    target = stats_in[2:3, :].astype(jnp.int32)
+    target = target_in[...]
 
     total = lax.fori_loop(
         0, n, lambda b, t: t + jnp.sum(jnp.exp(sc[b] - top), axis=0, keepdims=True),
@@ -186,8 +195,6 @@
     for k in range(1, n):
         stat_copy(k, me).start()
     stats_g[me] = stats_out[...]
-    if full > 1:
-        ring_full(1, users_g, 0)
 
     gu[...] = jnp.zeros_like(gu)
 
@@ -199,6 +206,13 @@
         return carry
 
     lax.fori_loop(0, n, back_user, 0)
+
+    def step_users(h, carry):
+        ring_full(1, users_g, h)
+        return carry
+
+    if full > 2:
+        lax.fori_loop(1, full - 1, step_users, 0)
     grad_user = gu[...].astype(BF16)
     back = mm(grad_user, w2[...], 1, 1)
     pre = pre_buf[...]
@@ -217,6 +231,8 @@
 
     for k in range(1, ng):
         d1_copy(k).start()
+    if full > 0:
+        ring_turn(1, users_g, full - 1)
 
     for k in range(1, n):
         stat_copy(k, lax.rem(me + n - k, n)).wait_recv()
@@ -231,22 +247,13 @@
         gi[...] += mm(ds, users_g[b], 1, 0)
 
     back_item(me)
-    if full > 1:
-        for b in behind(0):
-            back_item(b)
-
-    def step_users(h, carry):
-        ring_full(1, users_g, h)
+
+    def step_items_back(h, carry):
         for b in behind(h):
             back_item(b)
         return carry
 
-    if full > 0:
-        if full > 2:
-            lax.fori_loop(1, full - 1, step_users, 0)
-        ring_turn(1, users_g, full - 1)
-        for b in behind(full - 1):
-            back_item(b)
+    lax.fori_loop(0, full, step_items_back, 0)
 
     piece = quarter // n
     for k in range(1, ng):
@@ -286,8 +293,8 @@
     one = s2_send[me]
     for k in range(1, n):
         one = one + s2_recv[k - 1]
-    s3_send[...] = one
-    s3_recv[me] = one
+    s3_send[...] = one.astype(BF16)
+    s3_recv[me] = one.astype(BF16)
 
     for k in range(1, ng):
         gt_copy(k, lax.rem(grp + ng - k, ng)).wait_recv()
@@ -332,7 +339,7 @@
 
     for k in range(1, n):
         d3_copy(k, lax.rem(me + n - k, n)).wait_recv()
-    q_buf[...] = jnp.concatenate([s3_recv[q] for q in range(n)], axis=0).astype(BF16)
+    q_buf[...] = jnp.concatenate([s3_recv[q] for q in range(n)], axis=0)
     fin[grp] = q_buf[...]
 
     def d4_copy(k, slot):
@@ -352,9 +359,7 @@
     for k in range(1, ng):
         d4_copy(k, lax.rem(grp + ng - k, ng)).wait_recv()
     for q in range(ng):
-        first = q * quarter
-        out, base = (g_first, first) if first < dh else (g_second, first - dh)
-        out[base : base + quarter, :] = fin[q].astype(F32)
+        g_both[q * quarter : (q + 1) * quarter, :] = fin[q]
 
     ring_sent(0, items_g, items)
     ring_sent(1, users_g)
@@ -379,29 +384,20 @@
     cols = d // ng
     lows = 8
     span = ITEMS_DEV // lows
-    ids = item_owner[:, :, 0] * ITEMS_DEV + item_row
-    stats_in = jnp.concatenate(
-        [
-            jnp.zeros((1, m), F32), example_weight, positive.astype(F32), ids.astype(F32),
-            jnp.zeros((4, m), F32),
-        ],
-        axis=0,
-    )
     srows = -(-(3 + ng) // 8) * 8
     quarter = 2 * dh // ng
     piece = quarter // n
     hops = n // 2
     vmem = pl.BlockSpec(memory_space=pltpu.VMEM)
     sem = pltpu.SemaphoreType.DMA
-    table, g_first, g_second = pl.pallas_call(
+    table, g_both = pl.pallas_call(
         functools.partial(kernel, n, ng, lows),
         out_shape=(
             jax.ShapeDtypeStruct((cols, ITEMS_DEV), F32),
-            jax.ShapeDtypeStruct(w_first.shape, F32),
-            jax.ShapeDtypeStruct(w_second.shape, F32),
+            jax.ShapeDtypeStruct((2 * dh, d), BF16),
         ),
-        in_specs=[vmem] * 5,
-        out_specs=(vmem,) * 3,
+        in_specs=[vmem] * 8,
+        out_specs=(vmem,) * 2,
         scratch_shapes=[
             pltpu.VMEM((n, m, d), BF16),
             pltpu.VMEM((n, m, d), BF16),
@@ -421,11 +417,11 @@
             pltpu.VMEM((ng - 1, quarter, d), F32),
             pltpu.VMEM((n, piece, d), F32),
             pltpu.VMEM((n - 1, piece, d), F32),
-            pltpu.VMEM((piece, d), F32),
-            pltpu.VMEM((n, piece, d), F32),
+            pltpu.VMEM((piece, d), BF16),
+            pltpu.VMEM((n, piece, d), BF16),
             pltpu.VMEM((quarter, d), BF16),
             pltpu.VMEM((ng, quarter, d), BF16),
-            sem((3, 2, hops, 2)), sem((3, 2, hops, 2)),
+            sem((3, 2, hops, CHUNKS)), sem((3, 2, hops, CHUNKS)),
             sem((n - 1,)), sem((n - 1,)),
             sem((ng - 1,)), sem((ng - 1,)),
             sem((ng - 1,)), sem((ng - 1,)),
@@ -437,8 +433,11 @@
         compiler_params=pltpu.CompilerParams(
             collective_id=0, has_side_effects=True, vmem_limit_bytes=60 * 1024 * 1024
         ),
-    )(user_features[0], w_first, w_second, item_embed[0], stats_in)
-    return g_first, g_second, jnp.transpose(table)
+    )(
+        user_features[0], w_first, w_second, item_embed[0],
+        example_weight, positive, item_owner.reshape(1, m), item_row,
+    )
+    return g_both[:dh].astype(F32), g_both[dh:].astype(F32), jnp.transpose(table)
 
 
 def solution(mesh):

time: 70.4 us -> 64.9 us (0.922)
  local copies, waits for them, and re-layouts: 7.05 us -> 2.27 us
  Pallas kernels: 62.4 us -> 60 us
  other arithmetic: 0.01 us -> 1.79 us
    unnamed x13 -> x1, local copies, waits for them, and re-layouts: 6.43 us -> 2.27 us
    pallas_call x1, Pallas kernels: 62.4 us -> 60 us  [body(): pl.pallas_call(functools.partial(kernel, n, ng, lows), out_shape=(jax.Sha...]
    convert_element_type x2 -> x1, other arithmetic: 0.01 us -> 1.79 us  [body(): g_both[dh:].astype(F32)]
where the time goes in v2:
time: 64.9 us; the launch traced here: 64.7 us
  Pallas kernels  60 us (92%)
  local copies, waits for them, and re-layouts  2.27 us (3%)
  other arithmetic  1.79 us (3%)
    pallas_call x1, Pallas kernels, body(): pl.pallas_call(functools.partial(kernel, n, ng, lows), out_shape=(jax.Sha...  60 us
    unnamed x1, local copies, waits for them, and re-layouts  2.27 us
    convert_element_type x1, other arithmetic, body(): g_both[dh:].astype(F32)  1.79 us

profile of v2, /device:TPU:0, one launch (start us, length us, event | category | flops | bytes accessed | tf_op | source)
XLA Modules:
  0.0 64.7 jit_solution(6789407838951855885)
XLA Ops:
  0.6 60.0 %shard_map.103 = (f32[64,4096]{1,0:T(8,128)}, bf16[512,256]{1,0:T(8,128)(2,1)}) custom-call(bf16[256,256]{1,0:T(8,128)(2,1)} %bitcast.5, bf16[256,256]{1,0:T(8,128)(2,1)} %w1.1, bf16[256,256]{1,0:T(8,128)(2,1)} %w2.1, bf16[256,256]{1,0:T(8,128)(2,1)} %bitcast.6, f32[1,256]{1,0:T(1,128)} %weight_in.1, s32[1,256]{1,0:T(1,128)} %target_in.1, s32[1,256]{1,0:T(1,128)} %bitcast.7, ...), custom_call_target="tpu_custom_call" | custom-call | tf_op jit(solution)/shard_map/pallas_call | solution.py:393
  60.7 1.8 %slice_convert_fusion = (f32[256,256]{1,0:T(8,128)}, f32[256,256]{1,0:T(8,128)}) fusion(bf16[512,256]{1,0:T(8,128)(2,1)} %get-tuple-element.5), kind=kLoop, calls=%fused_computation | loop fusion | flops 131072 | bytes 786432 | tf_op jit(solution)/shard_map/convert_element_type | solution.py:440
  62.5 2.3 %copy.12 = f32[4096,64]{0,1:T(8,128)} copy(f32[4096,64]{0,1:T(8,128)} %bitcast.4) | data formatting | bytes 2097152
